TPU v7x, 512 devices: a whole 4x8x8 slice. The times are simulated.
512 devices in a mesh: layer: 4 (over x), row: 16 (over z, core), col: 8 (over y).
Axes of the slice: x: 4, y: 8, z: 8, core: 2. Of those that a mesh axis runs over, the one named last changes fastest.
Arguments:
- sources: bfloat16 [4, 96, 12288], P('layer', 'col', 'row'), may hold values from -6 to 6
- transmission: bfloat16 [4, 12288, 12288], P('layer', 'row', 'col'), may hold values from -0.0546875 to 0.0546875
- reflection: bfloat16 [4, 12288, 12288], P('layer', 'row', 'col'), may hold values from -0.02734375 to 0.02734375
Outputs:
- upgoing: bfloat16 [4, 96, 12288], P('layer', 'col', 'row')
All inputs are finite; a program needn't handle non-finite values.
Results may differ from a plain program's by a relative error of at most 0.012.
Values may be sent and summed in bfloat16 or wider, within the bound.
No kernel may reach another device: no remote copies, remote signals or barrier semaphores. Data moves between devices by JAX's collectives and lax.ppermute only.
A program may use at most 64 MiB of HBM per device.

v0:
```python
import jax
import jax.numpy as jnp
from jax import lax
from jax.sharding import PartitionSpec as P


def broadcast(array, axis, root):
    return lax.dynamic_index_in_dim(lax.all_gather(array, axis), root, 0, keepdims=False)


def copy_for_each(array, axis):
    length = lax.axis_size(axis)
    return lax.all_to_all(
        jnp.broadcast_to(array[None], (length, *array.shape)), axis, 0, 0, tiled=True
    )


def laid_out(tiles, dim):
    tiles = jnp.moveaxis(tiles, 0, dim)
    dims = tiles.shape
    return tiles.reshape(*dims[:dim], dims[dim] * dims[dim + 1], *dims[dim + 2 :])


def gather_directly(array, axis, dim):
    tiles = copy_for_each(array, axis)
    return laid_out(tiles, dim)


def in_blocks(array, dim, length):
    before, after = (array.shape[:dim], array.shape[dim + 1 :])
    return jnp.moveaxis(array.reshape(*before, length, -1, *after), dim, 0)


def summed_on_arrival(array, axis, dim):
    tiles = in_blocks(array, dim, lax.axis_size(axis))
    arrived = lax.all_to_all(tiles, axis, split_axis=0, concat_axis=0, tiled=True)
    return arrived.sum(axis=0)


def passed_along(array, axis, by):
    length = lax.axis_size(axis)
    pairs = [(i, i + by) for i in range(length) if 0 <= i + by < length]
    return lax.ppermute(array, axis, pairs)


def widen(narrow_traces, col_index, row_ratio):
    pieces = []
    for half in range(row_ratio):
        pieces.append(broadcast(narrow_traces, "row", row_ratio * col_index + half))
    return jnp.concatenate(pieces, axis=1)


def shrink(wide_traces, row_index, row_ratio, row_width):
    own_part = lax.dynamic_slice_in_dim(
        wide_traces, row_index % row_ratio * row_width, row_width, 1
    )
    return broadcast(own_part, "col", row_index // row_ratio)


def per_device(sources, transmission, reflection):
    layer_count = lax.axis_size("layer")
    row_ratio = lax.axis_size("row") // lax.axis_size("col")
    row_index = lax.axis_index("row")
    col_index = lax.axis_index("col")
    layer_index = lax.axis_index("layer")
    trans_tile = transmission[0]
    reflect_tile = reflection[0]
    row_width = trans_tile.shape[0]
    col_width = trans_tile.shape[1]
    source_narrow = gather_directly(sources[0], "col", 0)
    source_wide = widen(source_narrow, col_index, row_ratio)
    trace_count = source_narrow.shape[0]
    incoming_wide = jnp.zeros((trace_count, col_width), jnp.bfloat16)
    incoming_narrow = jnp.zeros((trace_count, row_width), jnp.bfloat16)
    incident_wide = source_wide
    down_wide = incoming_wide
    for step in range(layer_count):
        incident_narrow = (
            incoming_narrow.astype(jnp.float32) + source_narrow.astype(jnp.float32)
        ).astype(jnp.bfloat16)
        partial_value = jnp.dot(incident_narrow, trans_tile, preferred_element_type=jnp.float32)
        down_share = summed_on_arrival(partial_value, "row", 0).astype(jnp.bfloat16)
        down_wide = lax.all_gather(down_share, "row", axis=0, tiled=True)
        incoming_narrow = passed_along(
            shrink(down_wide, row_index, row_ratio, row_width), "layer", 1
        )
        if step == layer_count - 1:
            incident_wide = widen(incident_narrow, col_index, row_ratio)
    contract = (((1,), (1,)), ((), ()))
    upward_wide = down_wide
    result = None
    for step in range(layer_count):
        passed = lax.dot_general(
            upward_wide, trans_tile, contract, preferred_element_type=jnp.float32
        )
        bounced = lax.dot_general(
            incident_wide, reflect_tile, contract, preferred_element_type=jnp.float32
        )
        result = summed_on_arrival(passed + bounced, "col", 0).astype(jnp.bfloat16)
        if step < layer_count - 1:
            gathered = gather_directly(result, "col", 0)
            arrived = widen(passed_along(gathered, "layer", -1), col_index, row_ratio)
            upward_wide = jnp.where(layer_index == layer_count - 1, down_wide, arrived)
    return result[None]


def solution(mesh):
    return jax.shard_map(
        per_device,
        mesh=mesh,
        in_specs=(P("layer", "col", "row"), P("layer", "row", "col"), P("layer", "row", "col")),
        out_specs=P("layer", "col", "row"),
        check_vma=False,
    )
```

profile of v0, /device:TPU:1, one launch (start us, length us, event | category | flops | bytes accessed | tf_op | source)
XLA Modules:
  0.0 637.7 jit_solution(3604503876795294385)
XLA Ops:
  6.5 0.9 broadcast_in_dim.11
  7.4 16.2 %all_to_all.60 = bf16[8,12,768]{2,1,0:T(8,128)(2,1)S(1)} all-to-all(bf16[8,12,768]{2,1,0:T(8,128)(2,1)S(1)} %broadcast_in_dim.11), channel_id=1, replica_groups=mesh['layer'=4,'row'=16,'col'=8] {'col'}, dimensions={0} | all-to-all | bytes 294912 | tf_op jit(solution)/shard_map/all_to_all | solution.py:13
  24.2 1.3 copy.9
  25.4 13.0 %all-to-all-start.1 = ((f32[16,6,1536]{2,1,0:T(8,128)}), f32[16,6,1536]{2,1,0:T(8,128)S(1)}, u32[]{:S(2)}, u32[]{:S(2)}) async-start(f32[16,6,1536]{2,1,0:T(8,128)} %copy.9), calls=%async_computation.1 | async-start | bytes 1572864 | tf_op jit(solution)/shard_map/all_to_all | solution.py:36
  38.5 22.7 %all-to-all-done.1 = f32[16,6,1536]{2,1,0:T(8,128)S(1)} async-done(((f32[16,6,1536]{2,1,0:T(8,128)}), f32[16,6,1536]{2,1,0:T(8,128)S(1)}, u32[]{:S(2)}, u32[]{:S(2)}) %all-to-all-start.1) | async-done | bytes 589856 | tf_op jit(solution)/shard_map/all_to_all | solution.py:36
  61.3 15.5 %all-gather.7 = bf16[16,6,1536]{2,1,0:T(8,128)(2,1)S(1)} all-gather(bf16[1,6,1536]{2,1,0:T(8,128)(2,1)S(1)} %bitcast.75), channel_id=1, replica_groups=mesh['layer'=4,'row'=16,'col'=8] {'row'}, dimensions={0}, use_global_device_ids=true | all-gather | bytes 313344 | tf_op jit(solution)/shard_map/all_gather | solution.py:83
  76.9 0.7 constant_dynamic-slice_fusion.2
  77.7 30.1 %all-gather.19.cloned.1.call-done = bf16[768,768]{1,0:T(8,128)(2,1)} async-done(((bf16[96,768]{1,0:T(8,128)(2,1)}), bf16[768,768]{1,0:T(8,128)(2,1)}) %all-gather.19.cloned.1.call-update) | async-done | bytes 1179664 | tf_op jit(solution)/shard_map/all_gather | solution.py:8
  107.8 0.9 dynamic-slice_bitcast_fusion.10
  108.7 3.1 collective-permute-start
  111.9 2.0 collective-permute-done
  114.9 36.2 %all_to_all.61 = f32[16,6,1536]{2,1,0:T(8,128)S(1)} all-to-all(f32[16,6,1536]{2,1,0:T(8,128)S(1)} %copy.11), channel_id=1, replica_groups=mesh['layer'=4,'row'=16,'col'=8] {'row'}, dimensions={0} | all-to-all | bytes 1179648 | tf_op jit(solution)/shard_map/all_to_all | solution.py:36
  151.1 15.5 %all-gather.8 = bf16[16,6,1536]{2,1,0:T(8,128)(2,1)S(1)} all-gather(bf16[1,6,1536]{2,1,0:T(8,128)(2,1)S(1)} %bitcast.76), channel_id=1, replica_groups=mesh['layer'=4,'row'=16,'col'=8] {'row'}, dimensions={0}, use_global_device_ids=true | all-gather | bytes 313344 | tf_op jit(solution)/shard_map/all_gather | solution.py:83
  166.7 0.7 constant_dynamic-slice_fusion.1
  167.5 33.7 %all-gather.21.cloned.1.call-done = bf16[768,768]{1,0:T(8,128)(2,1)} async-done(((bf16[96,768]{1,0:T(8,128)(2,1)}), bf16[768,768]{1,0:T(8,128)(2,1)}) %all-gather.21.cloned.1.call-update) | async-done | bytes 1179664 | tf_op jit(solution)/shard_map/all_gather | solution.py:8
  201.2 0.9 dynamic-slice_bitcast_fusion.9
  202.1 3.1 collective-permute-start.1
  205.2 2.1 collective-permute-done.1
  208.2 36.2 %all_to_all.62 = f32[16,6,1536]{2,1,0:T(8,128)S(1)} all-to-all(f32[16,6,1536]{2,1,0:T(8,128)S(1)} %copy.13), channel_id=1, replica_groups=mesh['layer'=4,'row'=16,'col'=8] {'row'}, dimensions={0} | all-to-all | bytes 1179648 | tf_op jit(solution)/shard_map/all_to_all | solution.py:36
  244.5 15.5 %all-gather.9 = bf16[16,6,1536]{2,1,0:T(8,128)(2,1)S(1)} all-gather(bf16[1,6,1536]{2,1,0:T(8,128)(2,1)S(1)} %bitcast.77), channel_id=1, replica_groups=mesh['layer'=4,'row'=16,'col'=8] {'row'}, dimensions={0}, use_global_device_ids=true | all-gather | bytes 313344 | tf_op jit(solution)/shard_map/all_gather | solution.py:83
  260.1 0.7 constant_dynamic-slice_fusion
  260.9 33.7 %all-gather.23.cloned.1.call-done = bf16[768,768]{1,0:T(8,128)(2,1)} async-done(((bf16[96,768]{1,0:T(8,128)(2,1)}), bf16[768,768]{1,0:T(8,128)(2,1)}) %all-gather.23.cloned.1.call-update) | async-done | bytes 1179664 | tf_op jit(solution)/shard_map/all_gather | solution.py:8
  294.5 0.9 dynamic-slice_bitcast_fusion.8
  295.5 3.1 collective-permute-start.2
  298.6 2.1 collective-permute-done.2
  300.6 0.7 add_convert_fusion
  301.4 1.0 dot_general.41
  302.3 0.5 fusion.2
  302.9 1.3 copy.15
  304.1 13.5 %all-to-all-start.4 = ((f32[16,6,1536]{2,1,0:T(8,128)}), f32[16,6,1536]{2,1,0:T(8,128)S(1)}, u32[]{:S(2)}, u32[]{:S(2)}) async-start(f32[16,6,1536]{2,1,0:T(8,128)} %copy.15), calls=%async_computation.4 | async-start | bytes 1572864 | tf_op jit(solution)/shard_map/all_to_all | solution.py:36
  317.7 27.9 %all-to-all-done.4 = f32[16,6,1536]{2,1,0:T(8,128)S(1)} async-done(((f32[16,6,1536]{2,1,0:T(8,128)}), f32[16,6,1536]{2,1,0:T(8,128)S(1)}, u32[]{:S(2)}, u32[]{:S(2)}) %all-to-all-start.4) | async-done | bytes 589856 | tf_op jit(solution)/shard_map/all_to_all | solution.py:36
  345.6 16.3 %all-gather.10 = bf16[16,6,1536]{2,1,0:T(8,128)(2,1)S(1)} all-gather(bf16[1,6,1536]{2,1,0:T(8,128)(2,1)S(1)} %bitcast.78), channel_id=1, replica_groups=mesh['layer'=4,'row'=16,'col'=8] {'row'}, dimensions={0}, use_global_device_ids=true | all-gather | bytes 313344 | tf_op jit(solution)/shard_map/all_gather | solution.py:83
  362.0 1.0 dynamic-slice_bitcast_fusion.7
  363.0 2.5 fusion
  365.5 0.8 fusion.18
  366.4 0.8 reshape.51
  367.2 18.3 %all_to_all.63 = f32[8,12,768]{2,1,0:T(8,128)S(1)} all-to-all(f32[8,12,768]{2,1,0:T(8,128)} %reshape.51), channel_id=1, replica_groups=mesh['layer'=4,'row'=16,'col'=8] {'col'}, dimensions={0} | all-to-all | bytes 589824 | tf_op jit(solution)/shard_map/all_to_all | solution.py:36
  385.5 10.9 %all_to_all.64 = bf16[8,12,768]{2,1,0:T(8,128)(2,1)S(1)} all-to-all(bf16[8,12,768]{2,1,0:T(8,128)(2,1)S(1)} %broadcast_in_dim.12), channel_id=1, replica_groups=mesh['layer'=4,'row'=16,'col'=8] {'col'}, dimensions={0} | all-to-all | bytes 294912 | tf_op jit(solution)/shard_map/all_to_all | solution.py:13
  396.5 1.3 collective-permute-start.3
  397.8 5.7 collective-permute-done.3
  403.5 0.6 copy-done.1
  404.2 41.5 %all-gather.27.cloned.1.call-done = bf16[1536,768]{1,0:T(8,128)(2,1)} async-done(((bf16[96,768]{1,0:T(8,128)(2,1)}), bf16[1536,768]{1,0:T(8,128)(2,1)}) %all-gather.27.cloned.1.call-update) | async-done | bytes 2359312 | tf_op jit(solution)/shard_map/all_gather | solution.py:8
  445.8 1.0 dynamic-slice_bitcast_fusion.5
  446.8 0.9 fusion.27
  447.6 0.8 reshape.53
  448.4 20.5 %all_to_all.65 = f32[8,12,768]{2,1,0:T(8,128)S(1)} all-to-all(f32[8,12,768]{2,1,0:T(8,128)} %reshape.53), channel_id=1, replica_groups=mesh['layer'=4,'row'=16,'col'=8] {'col'}, dimensions={0} | all-to-all | bytes 589824 | tf_op jit(solution)/shard_map/all_to_all | solution.py:36
  469.0 10.9 %all_to_all.66 = bf16[8,12,768]{2,1,0:T(8,128)(2,1)S(1)} all-to-all(bf16[8,12,768]{2,1,0:T(8,128)(2,1)S(1)} %broadcast_in_dim.13), channel_id=1, replica_groups=mesh['layer'=4,'row'=16,'col'=8] {'col'}, dimensions={0} | all-to-all | bytes 294912 | tf_op jit(solution)/shard_map/all_to_all | solution.py:13
  479.9 1.3 collective-permute-start.4
  481.2 4.6 collective-permute-done.4
  485.8 0.6 copy-done.2
  486.5 40.3 %all-gather.29.cloned.1.call-done = bf16[1536,768]{1,0:T(8,128)(2,1)} async-done(((bf16[96,768]{1,0:T(8,128)(2,1)}), bf16[1536,768]{1,0:T(8,128)(2,1)}) %all-gather.29.cloned.1.call-update) | async-done | bytes 2359312 | tf_op jit(solution)/shard_map/all_gather | solution.py:8
  526.9 1.0 dynamic-slice_bitcast_fusion.3
  527.9 0.9 fusion.24
  528.7 0.8 reshape.55
  529.5 20.5 %all_to_all.67 = f32[8,12,768]{2,1,0:T(8,128)S(1)} all-to-all(f32[8,12,768]{2,1,0:T(8,128)} %reshape.55), channel_id=1, replica_groups=mesh['layer'=4,'row'=16,'col'=8] {'col'}, dimensions={0} | all-to-all | bytes 589824 | tf_op jit(solution)/shard_map/all_to_all | solution.py:36
  550.1 10.9 %all_to_all.68 = bf16[8,12,768]{2,1,0:T(8,128)(2,1)S(1)} all-to-all(bf16[8,12,768]{2,1,0:T(8,128)(2,1)S(1)} %broadcast_in_dim.14), channel_id=1, replica_groups=mesh['layer'=4,'row'=16,'col'=8] {'col'}, dimensions={0} | all-to-all | bytes 294912 | tf_op jit(solution)/shard_map/all_to_all | solution.py:13
  561.0 1.3 collective-permute-start.5
  562.3 4.6 collective-permute-done.5
  566.9 0.6 copy-done.3
  567.6 40.4 %all-gather.31.cloned.1.call-done = bf16[1536,768]{1,0:T(8,128)(2,1)} async-done(((bf16[96,768]{1,0:T(8,128)(2,1)}), bf16[1536,768]{1,0:T(8,128)(2,1)}) %all-gather.31.cloned.1.call-update) | async-done | bytes 2359312 | tf_op jit(solution)/shard_map/all_gather | solution.py:8
  608.0 1.0 dynamic-slice_bitcast_fusion.1
  609.0 0.9 fusion.21
  609.9 20.3 %all_to_all.69 = f32[8,12,768]{2,1,0:T(8,128)S(1)} all-to-all(f32[8,12,768]{2,1,0:T(8,128)S(1)} %reshape.57), channel_id=1, replica_groups=mesh['layer'=4,'row'=16,'col'=8] {'col'}, dimensions={0} | all-to-all | bytes 589824 | tf_op jit(solution)/shard_map/all_to_all | solution.py:36
  630.2 0.6 reduce_sum.79
  (49 shorter events, 3.8 us)
Async XLA Ops:
  6.5 17.1 %copy-start = (bf16[1,768,1536]{2,1,0:T(8,128)(2,1)S(1)}, bf16[1,768,1536]{2,1,0:T(8,128)(2,1)}, u32[]{:S(2)}) copy-start(bf16[1,768,1536]{2,1,0:T(8,128)(2,1)} %param.4) | copy-start | bytes 7077892
  25.4 35.8 %all-to-all-start.1 = ((f32[16,6,1536]{2,1,0:T(8,128)}), f32[16,6,1536]{2,1,0:T(8,128)S(1)}, u32[]{:S(2)}, u32[]{:S(2)}) async-start(f32[16,6,1536]{2,1,0:T(8,128)} %copy.9), calls=%async_computation.1 | async-start | bytes 1572864 | tf_op jit(solution)/shard_map/all_to_all | solution.py:36
  38.5 69.3 %all-gather.19.cloned.1.call-start = ((), (), s32[]{:S(2)}) async-start(), calls=%async_computation.12 | async-start | bytes 1327104 | tf_op jit(solution)/shard_map/all_gather | solution.py:8
  77.6 123.5 %all-gather.21.cloned.1.call-start = ((), (), s32[]{:S(2)}) async-start(), calls=%async_computation.13 | async-start | bytes 1327104 | tf_op jit(solution)/shard_map/all_gather | solution.py:8
  108.7 5.2 collective-permute-start
  167.5 127.1 %all-gather.23.cloned.1.call-start = ((), (), s32[]{:S(2)}) async-start(), calls=%async_computation.14 | async-start | bytes 1327104 | tf_op jit(solution)/shard_map/all_gather | solution.py:8
  202.1 5.2 collective-permute-start.1
  260.8 101.2 %all-gather.25.cloned.1.call-start = ((), (), s32[]{:S(2)}) async-start(), calls=%async_computation.15 | async-start | bytes 2506752 | tf_op jit(solution)/shard_map/all_gather | solution.py:8
  295.5 5.2 collective-permute-start.2
  304.1 41.4 %all-to-all-start.4 = ((f32[16,6,1536]{2,1,0:T(8,128)}), f32[16,6,1536]{2,1,0:T(8,128)S(1)}, u32[]{:S(2)}, u32[]{:S(2)}) async-start(f32[16,6,1536]{2,1,0:T(8,128)} %copy.15), calls=%async_computation.4 | async-start | bytes 1572864 | tf_op jit(solution)/shard_map/all_to_all | solution.py:36
  317.6 128.1 %all-gather.27.cloned.1.call-start = ((), (), s32[]{:S(2)}) async-start(), calls=%async_computation.16 | async-start | bytes 2506752 | tf_op jit(solution)/shard_map/all_gather | solution.py:8
  396.5 7.0 %collective-permute-start.3 = (bf16[96,768]{1,0:T(8,128)(2,1)S(1)}, bf16[96,768]{1,0:T(8,128)(2,1)S(1)}, u32[]{:S(2)}, u32[]{:S(2)}) collective-permute-start(bf16[96,768]{1,0:T(8,128)(2,1)S(1)} %reshape.52), channel_id=1, source_target_pairs={{128,0},{256,128},{384,256},{129,1},{257,129},{385,257},{130,2},{2... | collective-permute-start | bytes 442376 | tf_op jit(solution)/shard_map/ppermute | solution.py:43
  403.5 0.7 copy-start.1
  404.2 122.7 %all-gather.29.cloned.1.call-start = ((), (), s32[]{:S(2)}) async-start(), calls=%async_computation.17 | async-start | bytes 2506752 | tf_op jit(solution)/shard_map/all_gather | solution.py:8
  479.9 5.9 collective-permute-start.4
  485.8 0.7 copy-start.2
  486.5 121.5 %all-gather.31.cloned.1.call-start = ((), (), s32[]{:S(2)}) async-start(), calls=%async_computation.18 | async-start | bytes 2506752 | tf_op jit(solution)/shard_map/all_gather | solution.py:8
  561.0 5.9 collective-permute-start.5
  566.9 0.7 copy-start.3
Sparse Core Ops, SparseCore 0:
  77.7 30.0 all-gather.18
  167.6 33.5 all-gather.20
  260.9 33.5 all-gather.22
  301.5 56.9 all-gather.24
  404.3 41.4 all-gather.26
  486.6 40.2 all-gather.28
  567.7 40.2 all-gather.30
where the time goes:
time: 639 us; the launch traced here: 638 us
  waiting for transfers between devices  291 us (46%)
  blocking collectives  264 us (41%)
  starting transfers between devices  40 us (6%)
  local copies, waits for them, and re-layouts  19 us (3%)
  between operations  13.8 us (2%)
  matrix products  7.95 us (1%)
    all_gather x7, waiting for transfers between devices, broadcast(): lax.all_gather(array, axis)  220 us
    all_to_all x6, blocking collectives, summed_on_arrival(): lax.all_to_all(tiles, axis, split_axis=0, concat_axis=0, tiled=True)  152 us
    all_gather x4, blocking collectives, per_device(): down_wide = lax.all_gather(down_share, 'row', axis=0, tiled=True)  62.9 us
    all_to_all x2, waiting for transfers between devices, summed_on_arrival(): lax.all_to_all(tiles, axis, split_axis=0, concat_axis=0, tiled=True)  50.5 us
    all_to_all x4, blocking collectives, copy_for_each(): lax.all_to_all(jnp.broadcast_to(array[None], (length, *array.shape)), axi...  48.8 us
    all_to_all x2, starting transfers between devices, summed_on_arrival(): lax.all_to_all(tiles, axis, split_axis=0, concat_axis=0, tiled=True)  26.6 us
    ppermute x6, waiting for transfers between devices, passed_along(): return lax.ppermute(array, axis, pairs)  21.1 us
    ppermute x6, starting transfers between devices, passed_along(): return lax.ppermute(array, axis, pairs)  13.2 us
  transfers between devices with their start and end apart: 15, of which 14 were waited for; matrix products, arithmetic and copies ran while one was open for 0% of the time, Pallas kernels for 0%

commit v1 on v0

v1 whole, which is shorter than its diff:
```python
import jax
import jax.numpy as jnp
import numpy as np
from jax import lax
from jax.sharding import Mesh, PartitionSpec as P

BF16 = jnp.bfloat16
F32 = jnp.float32
GRID = ("layer", "z", "core", "col")
ROW = ("z", "core")


def copy_for_each(array, axis):
    length = lax.axis_size(axis)
    return lax.all_to_all(
        jnp.broadcast_to(array[None], (length, *array.shape)), axis, 0, 0, tiled=True
    )


def summed_on_arrival(tiles, axis):
    arrived = lax.all_to_all(tiles, axis, split_axis=0, concat_axis=0, tiled=True)
    return arrived.astype(F32).sum(axis=0).astype(BF16)


def per_device(sources, transmission, reflection):
    layers = lax.axis_size("layer")
    zs = lax.axis_size("z")
    cores = lax.axis_size("core")
    cols = lax.axis_size("col")
    half = zs // 2
    layer_index = lax.axis_index("layer")
    col_index = lax.axis_index("col")
    trans_tile = transmission[0]
    reflect_tile = reflection[0]
    row_width, col_width = trans_tile.shape
    few = sources.shape[1]
    traces = few * cols
    group, part = 2 * few, row_width // 2

    def flat(l, z, k, y):
        return ((l * zs + z) * cores + k) * cols + y

    def cells(layer_range):
        for l in layer_range:
            for z in range(zs):
                for k in range(cores):
                    for y in range(cols):
                        yield l, z, k, y

    down_pairs = [
        (flat(l, z, k, y), flat(l + 1, y, k, (z + half) % zs))
        for l, z, k, y in cells(range(layers - 1))
    ]
    back_pairs = [
        (flat(l, y, k, (z + half) % zs), flat(l, z, k, y)) for l, z, k, y in cells(range(layers))
    ]
    up_pairs = [
        (flat(l, z, k, y), flat(l - 1, (y + half) % zs, k, z))
        for l, z, k, y in cells(range(1, layers))
    ]

    def whole_block(pieces):
        tiles = pieces.reshape(cols // 2, 2, group, part)
        return tiles.transpose(0, 2, 1, 3).reshape(traces, row_width)

    source_narrow = copy_for_each(sources[0], "col").reshape(traces, row_width)
    incident = source_narrow
    share = None
    incident_share = None
    for step in range(layers):
        if step > 0:
            moved = lax.ppermute(share, GRID, down_pairs)
            incoming = whole_block(copy_for_each(moved, "col"))
            incident = (incoming.astype(F32) + source_narrow.astype(F32)).astype(BF16)
        if step == layers - 1:
            own = incident.reshape(cols // 2, group, 2, part).transpose(0, 2, 1, 3)
            own = own.reshape(cols, group, part)
            own = lax.dynamic_index_in_dim(own, col_index, 0, keepdims=False)
            incident_share = lax.ppermute(own, GRID, back_pairs)
        partial = jnp.dot(incident, trans_tile, preferred_element_type=F32).astype(BF16)
        tiles = partial.reshape(cols // 2, group, cores, 2, part).transpose(0, 3, 2, 1, 4)
        tiles = jnp.roll(tiles.reshape(zs, cores, group, part), -half, axis=0)
        share = summed_on_arrival(tiles.reshape(zs * cores, group, part), ROW)

    both = copy_for_each(jnp.stack([share, incident_share]), "z")
    both = jnp.roll(both, half, axis=0)
    both = lax.all_gather(both, "core")
    both = both.reshape(cores, cols // 2, 2, 2, group, part).transpose(3, 1, 4, 0, 2, 5)
    both = both.reshape(2, traces, col_width)
    contract = (((1,), (1,)), ((), ()))
    bounced = lax.dot_general(both[1], reflect_tile, contract, preferred_element_type=F32)
    upward = both[0]
    result = jnp.zeros((few, row_width), BF16)
    for step in range(layers):
        if step > 0:
            moved = lax.ppermute(newest, GRID, up_pairs)
            wide = jnp.roll(copy_for_each(moved, "z"), half, axis=0)
            wide = lax.all_gather(wide.reshape(traces, row_width), "core")
            upward = wide.transpose(1, 0, 2).reshape(traces, col_width)
        passed = lax.dot_general(upward, trans_tile, contract, preferred_element_type=F32)
        partial = (passed + bounced).astype(BF16)
        newest = summed_on_arrival(partial.reshape(cols, few, row_width), "col")
        result = jnp.where(layer_index == layers - 1 - step, newest, result)
    return result[None]


def solution(mesh):
    layers, rows, cols = mesh.devices.shape
    grid = Mesh(np.array(mesh.devices).reshape(layers, rows // 2, 2, cols), GRID)
    return jax.shard_map(
        per_device,
        mesh=grid,
        in_specs=(P("layer", "col", ROW), P("layer", ROW, "col"), P("layer", ROW, "col")),
        out_specs=P("layer", "col", ROW),
        check_vma=False,
    )
```

time: 639 us -> 320 us (0.50)
  waiting for transfers between devices: 291 us -> 50.2 us
  blocking collectives: 264 us -> 212 us
  local copies, waits for them, and re-layouts: 19 us -> 4.62 us
  between operations: 13.8 us -> 0.51 us
    all_gather x7 -> x0, waiting for transfers between devices: 220 us -> none  [broadcast(): lax.all_gather(array, axis)]
    all_to_all x6, blocking collectives: 152 us -> 104 us  [summed_on_arrival(): lax.all_to_all(tiles, axis, split_axis=0, concat_axis=0, tiled=True)]
    all_gather x4, blocking collectives: 62.9 us -> 20.4 us  [the longest x3 16.2 us: per_device(): wide = lax.all_gather(wide.reshape(traces, row_width), 'core')]
    all_to_all x4 -> x7, blocking collectives: 48.8 us -> 86.8 us  [copy_for_each(): lax.all_to_all(jnp.broadcast_to(array[None], (length, *array.shape)), axi...]
    all_to_all x2, waiting for transfers between devices: 50.5 us -> 15 us  [summed_on_arrival(): lax.all_to_all(tiles, axis, split_axis=0, concat_axis=0, tiled=True)]
    all_to_all x2, starting transfers between devices: 26.6 us -> 12.7 us  [summed_on_arrival(): lax.all_to_all(tiles, axis, split_axis=0, concat_axis=0, tiled=True)]
    ppermute x6 -> x7, starting transfers between devices: 13.2 us -> 24.3 us  [the longest x3 13.2 us: per_device(): moved = lax.ppermute(share, GRID, down_pairs)]
    all_to_all x0 -> x1, waiting for transfers between devices: none -> 8.14 us  [copy_for_each(): lax.all_to_all(jnp.broadcast_to(array[None], (length, *array.shape)), axi...]
  transfers between devices with their start and end apart: 15 -> 10, of which waited for: 14 -> 9; matrix products, arithmetic and copies ran while one was open for 0% -> 0% of each run, Pallas kernels for 0% -> 0%
where the time goes in v1:
time: 320 us; the launch traced here: 318 us
  blocking collectives  212 us (66%)
  waiting for transfers between devices  50.2 us (16%)
  starting transfers between devices  40.4 us (13%)
  matrix products  7.95 us (2%)
  local copies, waits for them, and re-layouts  4.62 us (1%)
    all_to_all x6, blocking collectives, summed_on_arrival(): lax.all_to_all(tiles, axis, split_axis=0, concat_axis=0, tiled=True)  104 us
    all_to_all x7, blocking collectives, copy_for_each(): lax.all_to_all(jnp.broadcast_to(array[None], (length, *array.shape)), axi...  86.8 us
    ppermute x3, waiting for transfers between devices, per_device(): moved = lax.ppermute(newest, GRID, up_pairs)  24.4 us
    all_gather x3, blocking collectives, per_device(): wide = lax.all_gather(wide.reshape(traces, row_width), 'core')  16.2 us
    all_to_all x2, waiting for transfers between devices, summed_on_arrival(): lax.all_to_all(tiles, axis, split_axis=0, concat_axis=0, tiled=True)  15 us
    ppermute x3, starting transfers between devices, per_device(): moved = lax.ppermute(share, GRID, down_pairs)  13.2 us
    all_to_all x2, starting transfers between devices, summed_on_arrival(): lax.all_to_all(tiles, axis, split_axis=0, concat_axis=0, tiled=True)  12.7 us
    all_to_all x1, waiting for transfers between devices, copy_for_each(): lax.all_to_all(jnp.broadcast_to(array[None], (length, *array.shape)), axi...  8.14 us
  transfers between devices with their start and end apart: 10, of which 9 were waited for; matrix products, arithmetic and copies ran while one was open for 0% of the time, Pallas kernels for 0%

profile of v1, /device:TPU:1, one launch (start us, length us, event | category | flops | bytes accessed | tf_op | source)
XLA Modules:
  0.0 317.6 jit_solution(17602662835237828083)
XLA Ops:
  0.0 0.9 broadcast_in_dim.21
  0.9 16.2 %all_to_all.80 = bf16[8,12,768]{2,1,0:T(8,128)(2,1)S(1)} all-to-all(bf16[8,12,768]{2,1,0:T(8,128)(2,1)S(1)} %broadcast_in_dim.21), channel_id=1, replica_groups=mesh['layer'=4,'z'=8,'core'=2,'col'=8] {'col'}, dimensions={0} | all-to-all | bytes 294912 | tf_op jit(solution)/shard_map/all_to_all | solution.py:15
  17.1 0.5 fusion.18
  17.6 0.1 reshape.138
  17.8 25.1 %all_to_all.81 = bf16[16,24,384]{2,1,0:T(8,128)(2,1)S(1)} all-to-all(bf16[16,24,384]{2,1,0:T(8,128)(2,1)S(1)} %bitcast.137), channel_id=1, replica_groups=mesh['layer'=4,'z'=8,'core'=2,'col'=8] {'z','core'}, dimensions={0} | all-to-all | bytes 589824 | tf_op jit(solution)/shard_map/all_to_all | solution.py:21
  43.0 3.1 collective-permute-start
  46.1 0.9 collective-permute-done
  47.0 0.7 broadcast_in_dim.22
  47.7 3.4 %all-to-all-start.2 = ((bf16[8,24,384]{2,1,0:T(8,128)(2,1)}), bf16[8,24,384]{2,1,0:T(8,128)(2,1)S(1)}, u32[]{:S(2)}, u32[]{:S(2)}) async-start(bf16[8,24,384]{2,1,0:T(8,128)(2,1)} %broadcast_in_dim.22), calls=%async_computation.2 | async-start | bytes 294912 | tf_op jit(solution)/shard_map/all_to_all | solution.py:15
  51.1 0.2 reshape.155
  51.2 8.1 %all-to-all-done.2 = bf16[8,24,384]{2,1,0:T(8,128)(2,1)S(1)} async-done(((bf16[8,24,384]{2,1,0:T(8,128)(2,1)}), bf16[8,24,384]{2,1,0:T(8,128)(2,1)S(1)}, u32[]{:S(2)}, u32[]{:S(2)}) %all-to-all-start.2) | async-done | bytes 147488 | tf_op jit(solution)/shard_map/all_to_all | solution.py:15
  59.4 0.1 copy.31
  59.5 0.5 fusion.21
  60.1 0.1 reshape.140
  60.3 20.7 %all_to_all.82 = bf16[16,24,384]{2,1,0:T(8,128)(2,1)S(1)} all-to-all(bf16[16,24,384]{2,1,0:T(8,128)(2,1)S(1)} %bitcast.138), channel_id=1, replica_groups=mesh['layer'=4,'z'=8,'core'=2,'col'=8] {'z','core'}, dimensions={0} | all-to-all | bytes 589824 | tf_op jit(solution)/shard_map/all_to_all | solution.py:21
  81.0 5.4 %collective-permute-start.1 = (bf16[24,384]{1,0:T(8,128)(2,1)S(1)}, bf16[24,384]{1,0:T(8,128)(2,1)S(1)}, u32[]{:S(2)}, u32[]{:S(2)}) collective-permute-start(bf16[24,384]{1,0:T(8,128)(2,1)S(1)} %reduce_sum.97), channel_id=1, source_target_pairs={{0,132},{1,148},{2,164},{3,180},{4,196},{5,212},{6,228},{7,244},{8... | collective-permute-start | bytes 55304 | tf_op jit(solution)/shard_map/ppermute | solution.py:72
  86.5 0.9 collective-permute-done.1
  87.4 10.3 %all_to_all.83 = bf16[8,24,384]{2,1,0:T(8,128)(2,1)S(1)} all-to-all(bf16[8,24,384]{2,1,0:T(8,128)(2,1)S(1)} %broadcast_in_dim.23), channel_id=1, replica_groups=mesh['layer'=4,'z'=8,'core'=2,'col'=8] {'col'}, dimensions={0} | all-to-all | bytes 294912 | tf_op jit(solution)/shard_map/all_to_all | solution.py:15
  97.7 0.2 fusion.57
  97.9 0.5 fusion.24
  98.4 0.1 reshape.142
  98.7 21.2 %all_to_all.84 = bf16[16,24,384]{2,1,0:T(8,128)(2,1)S(1)} all-to-all(bf16[16,24,384]{2,1,0:T(8,128)(2,1)S(1)} %bitcast.139), channel_id=1, replica_groups=mesh['layer'=4,'z'=8,'core'=2,'col'=8] {'z','core'}, dimensions={0} | all-to-all | bytes 589824 | tf_op jit(solution)/shard_map/all_to_all | solution.py:21
  120.0 4.7 %collective-permute-start.2 = (bf16[24,384]{1,0:T(8,128)(2,1)S(1)}, bf16[24,384]{1,0:T(8,128)(2,1)S(1)}, u32[]{:S(2)}, u32[]{:S(2)}) collective-permute-start(bf16[24,384]{1,0:T(8,128)(2,1)S(1)} %reduce_sum.98), channel_id=1, source_target_pairs={{0,132},{1,148},{2,164},{3,180},{4,196},{5,212},{6,228},{7,244},{8... | collective-permute-start | bytes 55304 | tf_op jit(solution)/shard_map/ppermute | solution.py:72
  124.7 0.9 collective-permute-done.2
  125.5 10.3 %all_to_all.85 = bf16[8,24,384]{2,1,0:T(8,128)(2,1)S(1)} all-to-all(bf16[8,24,384]{2,1,0:T(8,128)(2,1)S(1)} %broadcast_in_dim.24), channel_id=1, replica_groups=mesh['layer'=4,'z'=8,'core'=2,'col'=8] {'col'}, dimensions={0} | all-to-all | bytes 294912 | tf_op jit(solution)/shard_map/all_to_all | solution.py:15
  135.9 0.2 fusion.56
  136.1 0.5 fusion.27
  136.6 0.1 reshape.144
  136.8 0.7 pad_maximum_fusion.3
  137.5 9.3 %all-to-all-start.7 = ((bf16[16,24,384]{2,1,0:T(8,128)(2,1)}), bf16[16,24,384]{2,1,0:T(8,128)(2,1)S(1)}, u32[]{:S(2)}, u32[]{:S(2)}) async-start(bf16[16,24,384]{2,1,0:T(8,128)(2,1)} %bitcast.23), calls=%async_computation.7 | async-start | bytes 589824 | tf_op jit(solution)/shard_map/all_to_all | solution.py:21
  146.9 7.2 %collective-permute-start.3 = (bf16[24,384]{1,0:T(8,128)(2,1)S(1)}, bf16[24,384]{1,0:T(8,128)(2,1)S(1)}, u32[]{:S(2)}, u32[]{:S(2)}) collective-permute-start(bf16[24,384]{1,0:T(8,128)(2,1)S(1)} %dynamic-slice_bitcast_fusion), channel_id=1, source_target_pairs={{4,0},{20,1},{36,2},{52,3},{68,4},{84,5},{100,6},{116,7},{12,8},{2... | collective-permute-start | bytes 55304 | tf_op jit(solution)/shard_map/ppermute | solution.py:79
  154.0 5.1 %all-to-all-done.7 = bf16[16,24,384]{2,1,0:T(8,128)(2,1)S(1)} async-done(((bf16[16,24,384]{2,1,0:T(8,128)(2,1)}), bf16[16,24,384]{2,1,0:T(8,128)(2,1)S(1)}, u32[]{:S(2)}, u32[]{:S(2)}) %all-to-all-start.7) | async-done | bytes 294944 | tf_op jit(solution)/shard_map/all_to_all | solution.py:21
  159.2 0.0 collective-permute-done.3
  159.2 15.6 %all_to_all.86 = bf16[8,2,24,384]{3,2,1,0:T(8,128)(2,1)S(1)} all-to-all(bf16[8,2,24,384]{3,2,1,0:T(8,128)(2,1)S(1)} %broadcast_in_dim.25), channel_id=1, replica_groups=mesh['layer'=4,'z'=8,'core'=2,'col'=8] {'z'}, dimensions={0} | all-to-all | bytes 589824 | tf_op jit(solution)/shard_map/all_to_all | solution.py:15
  174.9 4.2 %all-gather = bf16[16,2,24,384]{3,2,1,0:T(8,128)(2,1)S(1)} all-gather(bf16[8,2,24,384]{3,2,1,0:T(8,128)(2,1)S(1)} %pad_maximum_fusion.4), channel_id=2, replica_groups=mesh['layer'=4,'z'=8,'core'=2,'col'=8] {'core'}, dimensions={0}, use_global_device_ids=true | all-gather | bytes 884736 | tf_op jit(solution)/shard_map/all_gather | solution.py:87
  179.1 0.1 fusion.58
  179.2 0.2 copy.39
  179.4 0.2 squeeze.19
  179.6 0.2 copy.38
  179.8 0.2 squeeze.18
  180.0 2.5 fusion
  182.5 0.9 fusion.51
  183.4 12.4 %all_to_all.87 = bf16[8,12,768]{2,1,0:T(8,128)(2,1)S(1)} all-to-all(bf16[8,12,768]{2,1,0:T(8,128)(2,1)S(1)} %reshape.148), channel_id=1, replica_groups=mesh['layer'=4,'z'=8,'core'=2,'col'=8] {'col'}, dimensions={0} | all-to-all | bytes 294912 | tf_op jit(solution)/shard_map/all_to_all | solution.py:21
  195.9 1.3 collective-permute-start.4
  197.2 8.2 %collective-permute-done.4 = bf16[12,768]{1,0:T(8,128)(2,1)S(1)} collective-permute-done((bf16[12,768]{1,0:T(8,128)(2,1)S(1)}, bf16[12,768]{1,0:T(8,128)(2,1)S(1)}, u32[]{:S(2)}, u32[]{:S(2)}) %collective-permute-start.4) | collective-permute-done | bytes 18464 | tf_op jit(solution)/shard_map/ppermute | solution.py:96
  205.4 12.4 %all_to_all.88 = bf16[8,12,768]{2,1,0:T(8,128)(2,1)S(1)} all-to-all(bf16[8,12,768]{2,1,0:T(8,128)(2,1)S(1)} %broadcast_in_dim.26), channel_id=1, replica_groups=mesh['layer'=4,'z'=8,'core'=2,'col'=8] {'z'}, dimensions={0} | all-to-all | bytes 294912 | tf_op jit(solution)/shard_map/all_to_all | solution.py:15
  217.9 5.6 %all_gather.17 = bf16[2,96,768]{2,1,0:T(8,128)(2,1)S(1)} all-gather(bf16[1,96,768]{2,1,0:T(8,128)(2,1)S(1)} %all_gather_reshape.9), channel_id=1, replica_groups=mesh['layer'=4,'z'=8,'core'=2,'col'=8] {'core'}, dimensions={0}, use_global_device_ids=true | all-gather | bytes 442368 | tf_op jit(solution)/shard_map/all_gather | solution.py:98
  223.6 0.8 fusion.48
  224.5 12.4 %all_to_all.89 = bf16[8,12,768]{2,1,0:T(8,128)(2,1)S(1)} all-to-all(bf16[8,12,768]{2,1,0:T(8,128)(2,1)S(1)} %reshape.150), channel_id=1, replica_groups=mesh['layer'=4,'z'=8,'core'=2,'col'=8] {'col'}, dimensions={0} | all-to-all | bytes 294912 | tf_op jit(solution)/shard_map/all_to_all | solution.py:21
  237.0 1.3 collective-permute-start.5
  238.3 8.1 %collective-permute-done.5 = bf16[12,768]{1,0:T(8,128)(2,1)S(1)} collective-permute-done((bf16[12,768]{1,0:T(8,128)(2,1)S(1)}, bf16[12,768]{1,0:T(8,128)(2,1)S(1)}, u32[]{:S(2)}, u32[]{:S(2)}) %collective-permute-start.5) | collective-permute-done | bytes 18464 | tf_op jit(solution)/shard_map/ppermute | solution.py:96
  246.4 11.0 %all_to_all.90 = bf16[8,12,768]{2,1,0:T(8,128)(2,1)S(1)} all-to-all(bf16[8,12,768]{2,1,0:T(8,128)(2,1)S(1)} %broadcast_in_dim.27), channel_id=1, replica_groups=mesh['layer'=4,'z'=8,'core'=2,'col'=8] {'z'}, dimensions={0} | all-to-all | bytes 294912 | tf_op jit(solution)/shard_map/all_to_all | solution.py:15
  257.5 5.3 %all_gather.18 = bf16[2,96,768]{2,1,0:T(8,128)(2,1)S(1)} all-gather(bf16[1,96,768]{2,1,0:T(8,128)(2,1)S(1)} %all_gather_reshape.10), channel_id=1, replica_groups=mesh['layer'=4,'z'=8,'core'=2,'col'=8] {'core'}, dimensions={0}, use_global_device_ids=true | all-gather | bytes 442368 | tf_op jit(solution)/shard_map/all_gather | solution.py:98
  262.8 0.8 fusion.45
  263.7 12.4 %all_to_all.91 = bf16[8,12,768]{2,1,0:T(8,128)(2,1)S(1)} all-to-all(bf16[8,12,768]{2,1,0:T(8,128)(2,1)S(1)} %reshape.152), channel_id=1, replica_groups=mesh['layer'=4,'z'=8,'core'=2,'col'=8] {'col'}, dimensions={0} | all-to-all | bytes 294912 | tf_op jit(solution)/shard_map/all_to_all | solution.py:21
  276.2 1.3 collective-permute-start.6
  277.5 8.1 %collective-permute-done.6 = bf16[12,768]{1,0:T(8,128)(2,1)S(1)} collective-permute-done((bf16[12,768]{1,0:T(8,128)(2,1)S(1)}, bf16[12,768]{1,0:T(8,128)(2,1)S(1)}, u32[]{:S(2)}, u32[]{:S(2)}) %collective-permute-start.6) | collective-permute-done | bytes 18464 | tf_op jit(solution)/shard_map/ppermute | solution.py:96
  285.6 11.0 %all_to_all.92 = bf16[8,12,768]{2,1,0:T(8,128)(2,1)S(1)} all-to-all(bf16[8,12,768]{2,1,0:T(8,128)(2,1)S(1)} %broadcast_in_dim.28), channel_id=1, replica_groups=mesh['layer'=4,'z'=8,'core'=2,'col'=8] {'z'}, dimensions={0} | all-to-all | bytes 294912 | tf_op jit(solution)/shard_map/all_to_all | solution.py:15
  296.8 5.3 %all_gather.19 = bf16[2,96,768]{2,1,0:T(8,128)(2,1)S(1)} all-gather(bf16[1,96,768]{2,1,0:T(8,128)(2,1)S(1)} %all_gather_reshape.11), channel_id=1, replica_groups=mesh['layer'=4,'z'=8,'core'=2,'col'=8] {'core'}, dimensions={0}, use_global_device_ids=true | all-gather | bytes 442368 | tf_op jit(solution)/shard_map/all_gather | solution.py:98
  302.1 0.8 fusion.42
  302.9 0.7 reshape.154
  303.6 3.4 %all-to-all-start.15 = ((bf16[8,12,768]{2,1,0:T(8,128)(2,1)}), bf16[8,12,768]{2,1,0:T(8,128)(2,1)S(1)}, u32[]{:S(2)}, u32[]{:S(2)}) async-start(bf16[8,12,768]{2,1,0:T(8,128)(2,1)} %reshape.154), calls=%async_computation.15 | async-start | bytes 393216 | tf_op jit(solution)/shard_map/all_to_all | solution.py:21
  307.0 9.9 %all-to-all-done.15 = bf16[8,12,768]{2,1,0:T(8,128)(2,1)S(1)} async-done(((bf16[8,12,768]{2,1,0:T(8,128)(2,1)}), bf16[8,12,768]{2,1,0:T(8,128)(2,1)S(1)}, u32[]{:S(2)}, u32[]{:S(2)}) %all-to-all-start.15) | async-done | bytes 147488 | tf_op jit(solution)/shard_map/all_to_all | solution.py:21
  317.0 0.6 select_bitcast_fusion
  (54 shorter events, 1.5 us)
Async XLA Ops:
  0.0 17.1 %copy-start = (bf16[1,768,1536]{2,1,0:T(8,128)(2,1)S(1)}, bf16[1,768,1536]{2,1,0:T(8,128)(2,1)}, u32[]{:S(2)}) copy-start(bf16[1,768,1536]{2,1,0:T(8,128)(2,1)} %param.4) | copy-start | bytes 7077892
  43.0 4.0 %collective-permute-start = (bf16[24,384]{1,0:T(8,128)(2,1)S(1)}, bf16[24,384]{1,0:T(8,128)(2,1)S(1)}, u32[]{:S(2)}, u32[]{:S(2)}) collective-permute-start(bf16[24,384]{1,0:T(8,128)(2,1)S(1)} %reduce_sum.96), channel_id=1, source_target_pairs={{0,132},{1,148},{2,164},{3,180},{4,196},{5,212},{6,228},{7,244},{8... | collective-permute-start | bytes 55304 | tf_op jit(solution)/shard_map/ppermute | solution.py:72
  47.7 11.7 %all-to-all-start.2 = ((bf16[8,24,384]{2,1,0:T(8,128)(2,1)}), bf16[8,24,384]{2,1,0:T(8,128)(2,1)S(1)}, u32[]{:S(2)}, u32[]{:S(2)}) async-start(bf16[8,24,384]{2,1,0:T(8,128)(2,1)} %broadcast_in_dim.22), calls=%async_computation.2 | async-start | bytes 294912 | tf_op jit(solution)/shard_map/all_to_all | solution.py:15
  81.0 6.3 %collective-permute-start.1 = (bf16[24,384]{1,0:T(8,128)(2,1)S(1)}, bf16[24,384]{1,0:T(8,128)(2,1)S(1)}, u32[]{:S(2)}, u32[]{:S(2)}) collective-permute-start(bf16[24,384]{1,0:T(8,128)(2,1)S(1)} %reduce_sum.97), channel_id=1, source_target_pairs={{0,132},{1,148},{2,164},{3,180},{4,196},{5,212},{6,228},{7,244},{8... | collective-permute-start | bytes 55304 | tf_op jit(solution)/shard_map/ppermute | solution.py:72
  120.0 5.6 %collective-permute-start.2 = (bf16[24,384]{1,0:T(8,128)(2,1)S(1)}, bf16[24,384]{1,0:T(8,128)(2,1)S(1)}, u32[]{:S(2)}, u32[]{:S(2)}) collective-permute-start(bf16[24,384]{1,0:T(8,128)(2,1)S(1)} %reduce_sum.98), channel_id=1, source_target_pairs={{0,132},{1,148},{2,164},{3,180},{4,196},{5,212},{6,228},{7,244},{8... | collective-permute-start | bytes 55304 | tf_op jit(solution)/shard_map/ppermute | solution.py:72
  137.5 21.6 %all-to-all-start.7 = ((bf16[16,24,384]{2,1,0:T(8,128)(2,1)}), bf16[16,24,384]{2,1,0:T(8,128)(2,1)S(1)}, u32[]{:S(2)}, u32[]{:S(2)}) async-start(bf16[16,24,384]{2,1,0:T(8,128)(2,1)} %bitcast.23), calls=%async_computation.7 | async-start | bytes 589824 | tf_op jit(solution)/shard_map/all_to_all | solution.py:21
  146.9 12.3 %collective-permute-start.3 = (bf16[24,384]{1,0:T(8,128)(2,1)S(1)}, bf16[24,384]{1,0:T(8,128)(2,1)S(1)}, u32[]{:S(2)}, u32[]{:S(2)}) collective-permute-start(bf16[24,384]{1,0:T(8,128)(2,1)S(1)} %dynamic-slice_bitcast_fusion), channel_id=1, source_target_pairs={{4,0},{20,1},{36,2},{52,3},{68,4},{84,5},{100,6},{116,7},{12,8},{2... | collective-permute-start | bytes 55304 | tf_op jit(solution)/shard_map/ppermute | solution.py:79
  195.9 9.5 %collective-permute-start.4 = (bf16[12,768]{1,0:T(8,128)(2,1)S(1)}, bf16[12,768]{1,0:T(8,128)(2,1)S(1)}, u32[]{:S(2)}, u32[]{:S(2)}) collective-permute-start(bf16[12,768]{1,0:T(8,128)(2,1)S(1)} %reduce_sum.100), channel_id=1, source_target_pairs={{128,64},{129,80},{130,96},{131,112},{132,0},{133,16},{134,32},{13... | collective-permute-start | bytes 55304 | tf_op jit(solution)/shard_map/ppermute | solution.py:96
  237.0 9.4 %collective-permute-start.5 = (bf16[12,768]{1,0:T(8,128)(2,1)S(1)}, bf16[12,768]{1,0:T(8,128)(2,1)S(1)}, u32[]{:S(2)}, u32[]{:S(2)}) collective-permute-start(bf16[12,768]{1,0:T(8,128)(2,1)S(1)} %reduce_sum.101), channel_id=1, source_target_pairs={{128,64},{129,80},{130,96},{131,112},{132,0},{133,16},{134,32},{13... | collective-permute-start | bytes 55304 | tf_op jit(solution)/shard_map/ppermute | solution.py:96
  276.2 9.4 %collective-permute-start.6 = (bf16[12,768]{1,0:T(8,128)(2,1)S(1)}, bf16[12,768]{1,0:T(8,128)(2,1)S(1)}, u32[]{:S(2)}, u32[]{:S(2)}) collective-permute-start(bf16[12,768]{1,0:T(8,128)(2,1)S(1)} %reduce_sum.102), channel_id=1, source_target_pairs={{128,64},{129,80},{130,96},{131,112},{132,0},{133,16},{134,32},{13... | collective-permute-start | bytes 55304 | tf_op jit(solution)/shard_map/ppermute | solution.py:96
  303.6 13.3 %all-to-all-start.15 = ((bf16[8,12,768]{2,1,0:T(8,128)(2,1)}), bf16[8,12,768]{2,1,0:T(8,128)(2,1)S(1)}, u32[]{:S(2)}, u32[]{:S(2)}) async-start(bf16[8,12,768]{2,1,0:T(8,128)(2,1)} %reshape.154), calls=%async_computation.15 | async-start | bytes 393216 | tf_op jit(solution)/shard_map/all_to_all | solution.py:21

commit v2 on v1

--- a/solution.py
+++ b/solution.py
@@ -20,6 +20,10 @@
 def summed_on_arrival(tiles, axis):
     arrived = lax.all_to_all(tiles, axis, split_axis=0, concat_axis=0, tiled=True)
     return arrived.astype(F32).sum(axis=0).astype(BF16)
+
+
+def added(a, b):
+    return (a.astype(F32) + b.astype(F32)).astype(BF16)
 
 
 def per_device(sources, transmission, reflection):
@@ -54,6 +58,9 @@
     back_pairs = [
         (flat(l, y, k, (z + half) % zs), flat(l, z, k, y)) for l, z, k, y in cells(range(layers))
     ]
+    below_pairs = [
+        (flat(l, z, k, y), flat(l + 1, z, k, y)) for l, z, k, y in cells(range(layers - 1))
+    ]
     up_pairs = [
         (flat(l, z, k, y), flat(l - 1, (y + half) % zs, k, z))
         for l, z, k, y in cells(range(1, layers))
@@ -63,44 +70,59 @@
         tiles = pieces.reshape(cols // 2, 2, group, part)
         return tiles.transpose(0, 2, 1, 3).reshape(traces, row_width)
 
-    source_narrow = copy_for_each(sources[0], "col").reshape(traces, row_width)
-    incident = source_narrow
-    share = None
-    incident_share = None
-    for step in range(layers):
-        if step > 0:
-            moved = lax.ppermute(share, GRID, down_pairs)
-            incoming = whole_block(copy_for_each(moved, "col"))
-            incident = (incoming.astype(F32) + source_narrow.astype(F32)).astype(BF16)
-        if step == layers - 1:
-            own = incident.reshape(cols // 2, group, 2, part).transpose(0, 2, 1, 3)
-            own = own.reshape(cols, group, part)
-            own = lax.dynamic_index_in_dim(own, col_index, 0, keepdims=False)
-            incident_share = lax.ppermute(own, GRID, back_pairs)
+    def share_of_down(incident):
         partial = jnp.dot(incident, trans_tile, preferred_element_type=F32).astype(BF16)
         tiles = partial.reshape(cols // 2, group, cores, 2, part).transpose(0, 3, 2, 1, 4)
         tiles = jnp.roll(tiles.reshape(zs, cores, group, part), -half, axis=0)
-        share = summed_on_arrival(tiles.reshape(zs * cores, group, part), ROW)
+        return summed_on_arrival(tiles.reshape(zs * cores, group, part), ROW)
 
-    both = copy_for_each(jnp.stack([share, incident_share]), "z")
+    def nothing(array, shape=(group, part)):
+        return jnp.zeros(shape, BF16)
+
+    source_narrow = copy_for_each(sources[0], "col").reshape(traces, row_width)
+
+    def on_arrival(moved):
+        return share_of_down(added(whole_block(copy_for_each(moved, "col")), source_narrow))
+
+    share = lax.cond(layer_index == 0, share_of_down, nothing, source_narrow)
+    own = source_narrow.reshape(cols // 2, group, 2, part).transpose(0, 2, 1, 3)
+    own = lax.dynamic_index_in_dim(own.reshape(cols, group, part), col_index, 0, keepdims=False)
+    source_share = None
+    above = jnp.zeros((group, part), BF16)
+    for step in range(1, layers):
+        moved = lax.ppermute(share, GRID, down_pairs)
+        if step == 1:
+            source_share = lax.ppermute(own, GRID, back_pairs)
+        above = jnp.where(layer_index == step, lax.ppermute(share, GRID, below_pairs), above)
+        share = lax.cond(layer_index == step, on_arrival, nothing, moved)
+
+    both = copy_for_each(jnp.stack([share, added(above, source_share)]), "z")
     both = jnp.roll(both, half, axis=0)
     both = lax.all_gather(both, "core")
     both = both.reshape(cores, cols // 2, 2, 2, group, part).transpose(3, 1, 4, 0, 2, 5)
     both = both.reshape(2, traces, col_width)
     contract = (((1,), (1,)), ((), ()))
     bounced = lax.dot_general(both[1], reflect_tile, contract, preferred_element_type=F32)
-    upward = both[0]
-    result = jnp.zeros((few, row_width), BF16)
-    for step in range(layers):
-        if step > 0:
-            moved = lax.ppermute(newest, GRID, up_pairs)
-            wide = jnp.roll(copy_for_each(moved, "z"), half, axis=0)
-            wide = lax.all_gather(wide.reshape(traces, row_width), "core")
-            upward = wide.transpose(1, 0, 2).reshape(traces, col_width)
+
+    def share_of_up(upward):
         passed = lax.dot_general(upward, trans_tile, contract, preferred_element_type=F32)
         partial = (passed + bounced).astype(BF16)
-        newest = summed_on_arrival(partial.reshape(cols, few, row_width), "col")
-        result = jnp.where(layer_index == layers - 1 - step, newest, result)
+        return summed_on_arrival(partial.reshape(cols, few, row_width), "col")
+
+    def on_return(moved):
+        wide = jnp.roll(copy_for_each(moved, "z"), half, axis=0)
+        wide = lax.all_gather(wide.reshape(traces, row_width), "core")
+        return share_of_up(wide.transpose(1, 0, 2).reshape(traces, col_width))
+
+    def nothing_up(array):
+        return nothing(array, (few, row_width))
+
+    result = newest = share_of_up(both[0])
+    for step in range(1, layers):
+        moved = lax.ppermute(newest, GRID, up_pairs)
+        turn = layer_index == layers - 1 - step
+        newest = lax.cond(turn, on_return, nothing_up, moved)
+        result = jnp.where(turn, newest, result)
     return result[None]
 
 

time: 320 us -> 312 us (0.975)
  blocking collectives: 212 us -> 87.5 us
  waiting for transfers between devices: 50.2 us -> 112 us
  starting transfers between devices: 40.4 us -> 100 us
    ppermute x3, waiting for transfers between devices: 24.4 us -> 101 us  [per_device(): moved = lax.ppermute(newest, GRID, up_pairs)]
    all_to_all x7 -> x2, blocking collectives: 86.8 us -> 27.3 us  [copy_for_each(): lax.all_to_all(jnp.broadcast_to(array[None], (length, *array.shape)), axi...]
    all_to_all x6 -> x3, blocking collectives: 104 us -> 50 us  [summed_on_arrival(): lax.all_to_all(tiles, axis, split_axis=0, concat_axis=0, tiled=True)]
    ppermute x1 -> x4, starting transfers between devices: 7.17 us -> 42.2 us  [the longest x3 35 us: per_device(): lax.ppermute(share, GRID, below_pairs)]
    ppermute x3, starting transfers between devices: 13.2 us -> 46.4 us  [per_device(): moved = lax.ppermute(share, GRID, down_pairs)]
    all_to_all x2 -> x0, waiting for transfers between devices: 15 us -> none  [summed_on_arrival(): lax.all_to_all(tiles, axis, split_axis=0, concat_axis=0, tiled=True)]
    all_to_all x2 -> x0, starting transfers between devices: 12.7 us -> none  [summed_on_arrival(): lax.all_to_all(tiles, axis, split_axis=0, concat_axis=0, tiled=True)]
    all_gather x3 -> x1, blocking collectives: 16.2 us -> 5.34 us  [on_return(): wide = lax.all_gather(wide.reshape(traces, row_width), 'core')]
  transfers between devices with their start and end apart: 10 -> 11, of which waited for: 9 -> 6; matrix products, arithmetic and copies ran while one was open for 0% -> 0% of each run, Pallas kernels for 0% -> 0%
where the time goes in v2:
time: 312 us; the launch traced here: 311 us
  waiting for transfers between devices  112 us (36%)
  starting transfers between devices  100 us (32%)
  blocking collectives  87.5 us (28%)
  matrix products  6.37 us (2%)
  local copies, waits for them, and re-layouts  3.82 us (1%)
    ppermute x3, waiting for transfers between devices, per_device(): moved = lax.ppermute(newest, GRID, up_pairs)  101 us
    all_to_all x3, blocking collectives, summed_on_arrival(): lax.all_to_all(tiles, axis, split_axis=0, concat_axis=0, tiled=True)  50 us
    ppermute x3, starting transfers between devices, per_device(): moved = lax.ppermute(share, GRID, down_pairs)  46.4 us
    ppermute x3, starting transfers between devices, per_device(): lax.ppermute(share, GRID, below_pairs)  35 us
    all_to_all x2, blocking collectives, copy_for_each(): lax.all_to_all(jnp.broadcast_to(array[None], (length, *array.shape)), axi...  27.3 us
    all_to_all x1, waiting for transfers between devices, copy_for_each(): lax.all_to_all(jnp.broadcast_to(array[None], (length, *array.shape)), axi...  8.73 us
    all_to_all x1, starting transfers between devices, copy_for_each(): lax.all_to_all(jnp.broadcast_to(array[None], (length, *array.shape)), axi...  7.64 us
    ppermute x1, starting transfers between devices, per_device(): source_share = lax.ppermute(own, GRID, back_pairs)  7.16 us
  transfers between devices with their start and end apart: 11, of which 6 were waited for; matrix products, arithmetic and copies ran while one was open for 0% of the time, Pallas kernels for 0%

profile of v2, /device:TPU:1, one launch (start us, length us, event | category | flops | bytes accessed | tf_op | source)
XLA Modules:
  0.0 310.8 jit_solution(8710218859428504777)
XLA Ops:
  0.0 0.0 copy-start
  0.0 1.6 broadcast_in_dim.33
  1.6 7.6 %all-to-all-start.13 = ((bf16[8,12,768]{2,1,0:T(8,128)(2,1)}), bf16[8,12,768]{2,1,0:T(8,128)(2,1)S(1)}, u32[]{:S(2)}, u32[]{:S(2)}) async-start(bf16[8,12,768]{2,1,0:T(8,128)(2,1)} %broadcast_in_dim.33), calls=%async_computation.13 | async-start | bytes 393216 | tf_op jit(solution)/shard_map/all_to_all | solution.py:15
  9.2 8.7 %all-to-all-done.13 = bf16[8,12,768]{2,1,0:T(8,128)(2,1)S(1)} async-done(((bf16[8,12,768]{2,1,0:T(8,128)(2,1)}), bf16[8,12,768]{2,1,0:T(8,128)(2,1)S(1)}, u32[]{:S(2)}, u32[]{:S(2)}) %all-to-all-start.13) | async-done | bytes 147488 | tf_op jit(solution)/shard_map/all_to_all | solution.py:15
  18.0 27.6 %conditional.7 = (bf16[24,384]{1,0:T(8,128)(2,1)S(1)}) conditional(s32[]{:T(128)} %convert_element_type.118, () %tuple.55, (bf16[96,768]{1,0:T(8,128)(2,1)S(1)}, bf16[768,1536]{1,0:T(8,128)(2,1)}) %tuple.86), branch_computations={%region_0.0_spmd, %region_1.3_spmd} | conditional | flops 226925568 | bytes 6064138 | solution.py:87
  18.0 2.2 convolution_convert_fusion
  20.2 0.1 reshape.84
  20.4 25.1 %all_to_all.67 = bf16[16,24,384]{2,1,0:T(8,128)(2,1)S(1)} all-to-all(bf16[16,24,384]{2,1,0:T(8,128)(2,1)S(1)} %bitcast.104), channel_id=1, replica_groups=mesh['layer'=4,'z'=8,'core'=2,'col'=8] {'z','core'}, dimensions={0} | all-to-all | bytes 589824 | tf_op jit(solution)/shard_map/cond/branch_1_fun/all_to_all | solution.py:21
  45.6 1.3 collective-permute-start
  46.9 0.9 collective-permute-done
  47.7 37.9 %collective-permute-start.1 = (bf16[24,384]{1,0:T(8,128)(2,1)S(1)}, bf16[24,384]{1,0:T(8,128)(2,1)S(1)}, u32[]{:S(2)}, u32[]{:S(2)}) collective-permute-start(bf16[24,384]{1,0:T(8,128)(2,1)S(1)} %get-tuple-element.106), channel_id=1, source_target_pairs={{0,132},{1,148},{2,164},{3,180},{4,196},{5,212},{6,228},{7,244},{8... | collective-permute-start | bytes 55304 | tf_op jit(solution)/shard_map/ppermute | solution.py:93
  85.6 1.9 collective-permute-start.5
  87.6 0.1 reshape_reshape.3
  87.7 0.0 collective-permute-done.1
  87.7 7.2 %collective-permute-start.2 = (bf16[24,384]{1,0:T(8,128)(2,1)S(1)}, bf16[24,384]{1,0:T(8,128)(2,1)S(1)}, u32[]{:S(2)}, u32[]{:S(2)}) collective-permute-start(bf16[24,384]{1,0:T(8,128)(2,1)S(1)} %get-tuple-element.107), channel_id=1, source_target_pairs={{0,132},{1,148},{2,164},{3,180},{4,196},{5,212},{6,228},{7,244},{8... | collective-permute-start | bytes 55304 | tf_op jit(solution)/shard_map/ppermute | solution.py:93
  95.0 7.2 %collective-permute-start.6 = (bf16[24,384]{1,0:T(8,128)(2,1)S(1)}, bf16[24,384]{1,0:T(8,128)(2,1)S(1)}, u32[]{:S(2)}, u32[]{:S(2)}) collective-permute-start(bf16[24,384]{1,0:T(8,128)(2,1)S(1)} %dynamic-slice_bitcast_fusion), channel_id=1, source_target_pairs={{4,0},{20,1},{36,2},{52,3},{68,4},{84,5},{100,6},{116,7},{12,8},{2... | collective-permute-start | bytes 55304 | tf_op jit(solution)/shard_map/ppermute | solution.py:95
  102.2 31.1 %collective-permute-start.4 = (bf16[24,384]{1,0:T(8,128)(2,1)S(1)}, bf16[24,384]{1,0:T(8,128)(2,1)S(1)}, u32[]{:S(2)}, u32[]{:S(2)}) collective-permute-start(bf16[24,384]{1,0:T(8,128)(2,1)S(1)} %get-tuple-element.106), channel_id=1, source_target_pairs={{0,128},{1,129},{2,130},{3,131},{4,132},{5,133},{6,134},{7,135},{8... | collective-permute-start | bytes 55304 | tf_op jit(solution)/shard_map/ppermute | solution.py:96
  133.3 1.9 collective-permute-start.3
  135.2 0.0 collective-permute-done.2
  135.3 0.0 collective-permute-done.5
  135.3 0.0 collective-permute-done.6
  135.3 0.0 collective-permute-done.4
  135.3 0.8 collective-permute-done.3
  136.2 12.8 %all_to_all.80 = bf16[8,2,24,384]{3,2,1,0:T(8,128)(2,1)S(1)} all-to-all(bf16[8,2,24,384]{3,2,1,0:T(8,128)(2,1)S(1)} %broadcast_in_dim.34), channel_id=1, replica_groups=mesh['layer'=4,'z'=8,'core'=2,'col'=8] {'z'}, dimensions={0} | all-to-all | bytes 589824 | tf_op jit(solution)/shard_map/all_to_all | solution.py:15
  149.1 4.9 %all-gather = bf16[16,2,24,384]{3,2,1,0:T(8,128)(2,1)S(1)} all-gather(bf16[8,2,24,384]{3,2,1,0:T(8,128)(2,1)S(1)} %pad_maximum_fusion.7), channel_id=2, replica_groups=mesh['layer'=4,'z'=8,'core'=2,'col'=8] {'core'}, dimensions={0}, use_global_device_ids=true | all-gather | bytes 884736 | tf_op jit(solution)/shard_map/all_gather | solution.py:101
  154.0 0.1 fusion.15
  154.1 0.2 copy.36
  154.3 0.2 squeeze.18
  154.5 0.2 copy.37
  154.8 0.2 squeeze.19
  155.0 0.0 copy-done
  155.0 0.0 copy-start.1
  155.0 0.8 fusion.3
  155.8 0.8 copy-done.1
  156.6 0.8 fusion.5
  157.5 12.4 %all_to_all.81 = bf16[8,12,768]{2,1,0:T(8,128)(2,1)S(1)} all-to-all(bf16[8,12,768]{2,1,0:T(8,128)(2,1)S(1)} %reshape.108), channel_id=1, replica_groups=mesh['layer'=4,'z'=8,'core'=2,'col'=8] {'col'}, dimensions={0} | all-to-all | bytes 294912 | tf_op jit(solution)/shard_map/all_to_all | solution.py:21
  170.0 1.3 collective-permute-start.7
  171.3 8.1 %collective-permute-done.7 = bf16[12,768]{1,0:T(8,128)(2,1)S(1)} collective-permute-done((bf16[12,768]{1,0:T(8,128)(2,1)S(1)}, bf16[12,768]{1,0:T(8,128)(2,1)S(1)}, u32[]{:S(2)}, u32[]{:S(2)}) %collective-permute-start.7) | collective-permute-done | bytes 18464 | tf_op jit(solution)/shard_map/ppermute | solution.py:122
  179.4 1.3 collective-permute-start.8
  180.7 8.1 %collective-permute-done.8 = bf16[12,768]{1,0:T(8,128)(2,1)S(1)} collective-permute-done((bf16[12,768]{1,0:T(8,128)(2,1)S(1)}, bf16[12,768]{1,0:T(8,128)(2,1)S(1)}, u32[]{:S(2)}, u32[]{:S(2)}) %collective-permute-start.8) | collective-permute-done | bytes 18464 | tf_op jit(solution)/shard_map/ppermute | solution.py:122
  188.7 1.3 collective-permute-start.9
  190.0 85.2 %collective-permute-done.9 = bf16[12,768]{1,0:T(8,128)(2,1)S(1)} collective-permute-done((bf16[12,768]{1,0:T(8,128)(2,1)S(1)}, bf16[12,768]{1,0:T(8,128)(2,1)S(1)}, u32[]{:S(2)}, u32[]{:S(2)}) %collective-permute-start.9) | collective-permute-done | bytes 18464 | tf_op jit(solution)/shard_map/ppermute | solution.py:122
  275.2 35.0 %conditional.13 = (bf16[12,768]{1,0:T(8,128)(2,1)S(1)}) conditional(s32[]{:T(128)} %convert_element_type.118, () %tuple.49, (bf16[12,768]{1,0:T(8,128)(2,1)S(1)}, bf16[768,1536]{1,0:T(8,128)(2,1)}, f32[96,768]{1,0:T(8,128)S(1)}) %tuple.92), branch_computations={%region_19.20_spmd, %region_20.22_spmd} | conditional | flops 226778112 | bytes 6230026 | solution.py:124
  275.2 14.5 %all_to_all.78 = bf16[8,12,768]{2,1,0:T(8,128)(2,1)S(1)} all-to-all(bf16[8,12,768]{2,1,0:T(8,128)(2,1)S(1)} %broadcast_in_dim.27), channel_id=1, replica_groups=mesh['layer'=4,'z'=8,'core'=2,'col'=8] {'z'}, dimensions={0} | all-to-all | bytes 294912 | tf_op jit(solution)/shard_map/cond/branch_1_fun/all_to_all | solution.py:15
  289.8 5.3 %all_gather.12 = bf16[2,96,768]{2,1,0:T(8,128)(2,1)S(1)} all-gather(bf16[1,96,768]{2,1,0:T(8,128)(2,1)S(1)} %reshape.98), channel_id=1, replica_groups=mesh['layer'=4,'z'=8,'core'=2,'col'=8] {'core'}, dimensions={0}, use_global_device_ids=true | all-gather | bytes 442368 | tf_op jit(solution)/shard_map/cond/branch_1_fun/all_gather | solution.py:114
  295.1 2.5 fusion.2
  297.7 12.4 %all_to_all.79 = bf16[8,12,768]{2,1,0:T(8,128)(2,1)S(1)} all-to-all(bf16[8,12,768]{2,1,0:T(8,128)(2,1)S(1)} %reshape.100), channel_id=1, replica_groups=mesh['layer'=4,'z'=8,'core'=2,'col'=8] {'col'}, dimensions={0} | all-to-all | bytes 294912 | tf_op jit(solution)/shard_map/cond/branch_1_fun/all_to_all | solution.py:21
  310.2 0.6 select_bitcast_fusion
  (31 shorter events, 0.7 us)
Async XLA Ops:
  0.0 155.0 %copy-start = (bf16[1,768,1536]{2,1,0:T(8,128)(2,1)S(1)}, bf16[1,768,1536]{2,1,0:T(8,128)(2,1)}, u32[]{:S(2)}) copy-start(bf16[1,768,1536]{2,1,0:T(8,128)(2,1)} %param.19) | copy-start | bytes 7077892
  1.6 16.4 %all-to-all-start.13 = ((bf16[8,12,768]{2,1,0:T(8,128)(2,1)}), bf16[8,12,768]{2,1,0:T(8,128)(2,1)S(1)}, u32[]{:S(2)}, u32[]{:S(2)}) async-start(bf16[8,12,768]{2,1,0:T(8,128)(2,1)} %broadcast_in_dim.33), calls=%async_computation.13 | async-start | bytes 393216 | tf_op jit(solution)/shard_map/all_to_all | solution.py:15
  45.6 2.2 collective-permute-start
  47.7 39.9 %collective-permute-start.1 = (bf16[24,384]{1,0:T(8,128)(2,1)S(1)}, bf16[24,384]{1,0:T(8,128)(2,1)S(1)}, u32[]{:S(2)}, u32[]{:S(2)}) collective-permute-start(bf16[24,384]{1,0:T(8,128)(2,1)S(1)} %get-tuple-element.106), channel_id=1, source_target_pairs={{0,132},{1,148},{2,164},{3,180},{4,196},{5,212},{6,228},{7,244},{8... | collective-permute-start | bytes 55304 | tf_op jit(solution)/shard_map/ppermute | solution.py:93
  85.6 49.7 %collective-permute-start.5 = (bf16[24,384]{1,0:T(8,128)(2,1)S(1)}, bf16[24,384]{1,0:T(8,128)(2,1)S(1)}, u32[]{:S(2)}, u32[]{:S(2)}) collective-permute-start(bf16[24,384]{1,0:T(8,128)(2,1)S(1)} %get-tuple-element.105), channel_id=1, source_target_pairs={{0,128},{1,129},{2,130},{3,131},{4,132},{5,133},{6,134},{7,135},{8... | collective-permute-start | bytes 55304 | tf_op jit(solution)/shard_map/ppermute | solution.py:96
  87.7 47.5 %collective-permute-start.2 = (bf16[24,384]{1,0:T(8,128)(2,1)S(1)}, bf16[24,384]{1,0:T(8,128)(2,1)S(1)}, u32[]{:S(2)}, u32[]{:S(2)}) collective-permute-start(bf16[24,384]{1,0:T(8,128)(2,1)S(1)} %get-tuple-element.107), channel_id=1, source_target_pairs={{0,132},{1,148},{2,164},{3,180},{4,196},{5,212},{6,228},{7,244},{8... | collective-permute-start | bytes 55304 | tf_op jit(solution)/shard_map/ppermute | solution.py:93
  95.0 40.3 %collective-permute-start.6 = (bf16[24,384]{1,0:T(8,128)(2,1)S(1)}, bf16[24,384]{1,0:T(8,128)(2,1)S(1)}, u32[]{:S(2)}, u32[]{:S(2)}) collective-permute-start(bf16[24,384]{1,0:T(8,128)(2,1)S(1)} %dynamic-slice_bitcast_fusion), channel_id=1, source_target_pairs={{4,0},{20,1},{36,2},{52,3},{68,4},{84,5},{100,6},{116,7},{12,8},{2... | collective-permute-start | bytes 55304 | tf_op jit(solution)/shard_map/ppermute | solution.py:95
  102.2 33.2 %collective-permute-start.4 = (bf16[24,384]{1,0:T(8,128)(2,1)S(1)}, bf16[24,384]{1,0:T(8,128)(2,1)S(1)}, u32[]{:S(2)}, u32[]{:S(2)}) collective-permute-start(bf16[24,384]{1,0:T(8,128)(2,1)S(1)} %get-tuple-element.106), channel_id=1, source_target_pairs={{0,128},{1,129},{2,130},{3,131},{4,132},{5,133},{6,134},{7,135},{8... | collective-permute-start | bytes 55304 | tf_op jit(solution)/shard_map/ppermute | solution.py:96
  133.3 2.8 collective-permute-start.3
  155.0 1.7 copy-start.1
  170.0 9.4 %collective-permute-start.7 = (bf16[12,768]{1,0:T(8,128)(2,1)S(1)}, bf16[12,768]{1,0:T(8,128)(2,1)S(1)}, u32[]{:S(2)}, u32[]{:S(2)}) collective-permute-start(bf16[12,768]{1,0:T(8,128)(2,1)S(1)} %reduce_sum.96), channel_id=1, source_target_pairs={{128,64},{129,80},{130,96},{131,112},{132,0},{133,16},{134,32},{13... | collective-permute-start | bytes 55304 | tf_op jit(solution)/shard_map/ppermute | solution.py:122
  179.4 9.4 %collective-permute-start.8 = (bf16[12,768]{1,0:T(8,128)(2,1)S(1)}, bf16[12,768]{1,0:T(8,128)(2,1)S(1)}, u32[]{:S(2)}, u32[]{:S(2)}) collective-permute-start(bf16[12,768]{1,0:T(8,128)(2,1)S(1)} %get-tuple-element.109), channel_id=1, source_target_pairs={{128,64},{129,80},{130,96},{131,112},{132,0},{133,16},{134,32},{13... | collective-permute-start | bytes 55304 | tf_op jit(solution)/shard_map/ppermute | solution.py:122
  188.7 86.4 %collective-permute-start.9 = (bf16[12,768]{1,0:T(8,128)(2,1)S(1)}, bf16[12,768]{1,0:T(8,128)(2,1)S(1)}, u32[]{:S(2)}, u32[]{:S(2)}) collective-permute-start(bf16[12,768]{1,0:T(8,128)(2,1)S(1)} %get-tuple-element.110), channel_id=1, source_target_pairs={{128,64},{129,80},{130,96},{131,112},{132,0},{133,16},{134,32},{13... | collective-permute-start | bytes 55304 | tf_op jit(solution)/shard_map/ppermute | solution.py:122
